TPU v7x, 8 devices: a whole 2x2x1 slice. The times are simulated.
8 devices in a mesh: ep: 2 (over z, y), dp: 4 (over x, core).
Axes of the slice: x: 2, y: 2, z: 1, core: 2. Of those that a mesh axis runs over, the one named last changes fastest.
Arguments:
- act_in: bfloat16 [16384, 448], P(('ep', 'dp'))
- grad_out: bfloat16 [16384, 448], P(('ep', 'dp'))
- slot_ids: int32 [2, 16384, 8], P(None, ('ep', 'dp'))
- gate_vals: float32 [2, 16384, 8], P(None, ('ep', 'dp'))
- w_dense: bfloat16 [2, 448, 448], replicated
- w_gate: bfloat16 [2, 64, 448, 320], P(None, 'ep')
- w_up: bfloat16 [2, 64, 448, 320], P(None, 'ep')
- w_down: bfloat16 [2, 64, 320, 448], P(None, 'ep')
- ws_gate: bfloat16 [2, 448, 2560], replicated
- ws_up: bfloat16 [2, 448, 2560], replicated
- ws_down: bfloat16 [2, 2560, 448], replicated
Outputs:
- output 1: bfloat16 [16384, 448], P(('ep', 'dp'))
- output 2: bfloat16 [2, 448, 448], replicated
- output 3: bfloat16 [2, 64, 448, 320], P(None, 'ep')
- output 4: bfloat16 [2, 64, 448, 320], P(None, 'ep')
- output 5: bfloat16 [2, 64, 320, 448], P(None, 'ep')
- output 6: bfloat16 [2, 448, 2560], replicated
- output 7: bfloat16 [2, 448, 2560], replicated
- output 8: bfloat16 [2, 2560, 448], replicated
All inputs are finite; a program needn't handle non-finite values.
Results may differ from a plain program's by a relative error of at most 0.02.
Values are sent between devices in bfloat16 or wider.
A program may use at most 1 GiB of HBM per device.

v0:
```python
import jax
import jax.numpy as jnp
from jax import lax
from jax.sharding import PartitionSpec as P

ALL_AXES = ("ep", "dp")


def silu_grad(pre_act):
    sigma = jax.nn.sigmoid(pre_act)
    return sigma * (1.0 + pre_act * (1.0 - sigma))


def contract_rows(left, right):
    return lax.dot_general(left, right, (((0,), (0,)), ((), ())), preferred_element_type=jnp.float32)


def contract_cols(left, right):
    return lax.dot_general(left, right, (((1,), (1,)), ((), ())), preferred_element_type=jnp.float32)


def layer_front(act, weights, slot_ids, ep_size):
    w_dense, w_gate, w_up, w_down, ws_gate, ws_up, ws_down = weights
    tokens, width = act.shape
    top = slot_ids.shape[1]
    local_exp = w_gate.shape[0]
    capacity = 2 * tokens * top // (local_exp * ep_size)
    dense_pre = jnp.dot(act, w_dense, preferred_element_type=jnp.float32)
    mixed = (act.astype(jnp.float32) + dense_pre).astype(jnp.bfloat16)
    slot_flat = slot_ids.reshape(tokens * top)
    copy_ids = jnp.arange(1, tokens * top + 1, dtype=jnp.int32)
    slot_owner = jnp.zeros((local_exp * ep_size * capacity,), jnp.int32).at[slot_flat].set(copy_ids)
    tok_owner = (slot_owner + top - 1) // top
    mixed_ext = jnp.concatenate([jnp.zeros((1, width), mixed.dtype), mixed], axis=0)
    send_buf = jnp.take(mixed_ext, tok_owner, axis=0).reshape(ep_size, local_exp, capacity, width)
    recv_rows = lax.all_to_all(send_buf, "ep", 0, 1).reshape(local_exp, ep_size * capacity, width)
    a_one = jnp.einsum("erd,edf->erf", recv_rows, w_gate, preferred_element_type=jnp.float32)
    a_three = jnp.einsum("erd,edf->erf", recv_rows, w_up, preferred_element_type=jnp.float32)
    hidden = (jax.nn.silu(a_one) * a_three).astype(jnp.bfloat16)
    s_one = jnp.dot(mixed, ws_gate, preferred_element_type=jnp.float32)
    s_three = jnp.dot(mixed, ws_up, preferred_element_type=jnp.float32)
    shared_hidden = (jax.nn.silu(s_one) * s_three).astype(jnp.bfloat16)
    return (act, mixed, slot_flat, slot_owner, recv_rows, a_one, a_three, hidden, s_one, s_three, shared_hidden)


def layer_finish(saved, weights, gate_vals, ep_size):
    act, mixed, slot_flat, slot_owner, recv_rows, a_one, a_three, hidden, s_one, s_three, shared_hidden = saved
    w_down = weights[3]
    ws_down = weights[6]
    tokens, width = mixed.shape
    top = gate_vals.shape[1]
    local_exp = hidden.shape[0]
    capacity = recv_rows.shape[1] // ep_size
    exp_out = jnp.einsum("erf,efd->erd", hidden, w_down, preferred_element_type=jnp.float32).astype(jnp.bfloat16)
    back_rows = lax.all_to_all(exp_out.reshape(local_exp, ep_size, capacity, width), "ep", 1, 0).reshape(local_exp * ep_size * capacity, width)
    picked = jnp.take(back_rows, slot_flat, axis=0).reshape(tokens, top, width)
    routed = jnp.sum(gate_vals[:, :, None] * picked.astype(jnp.float32), axis=1)
    shared_out = jnp.dot(shared_hidden, ws_down, preferred_element_type=jnp.float32)
    return (mixed.astype(jnp.float32) + routed + shared_out).astype(jnp.bfloat16)


def layer_backward(grad_y, saved, weights, gate_vals, ep_size):
    act, mixed, slot_flat, slot_owner, recv_rows, a_one, a_three, hidden, s_one, s_three, shared_hidden = saved
    w_dense, w_gate, w_up, w_down, ws_gate, ws_up, ws_down = weights
    tokens, width = grad_y.shape
    top = gate_vals.shape[1]
    local_exp = hidden.shape[0]
    capacity = recv_rows.shape[1] // ep_size
    grad_y32 = grad_y.astype(jnp.float32)
    grad_pick = (gate_vals[:, :, None] * grad_y32[:, None, :]).astype(jnp.bfloat16).reshape(tokens * top, width)
    grad_ext = jnp.concatenate([jnp.zeros((1, width), grad_pick.dtype), grad_pick], axis=0)
    send_grad = jnp.take(grad_ext, slot_owner, axis=0).reshape(ep_size, local_exp, capacity, width)
    grad_exp_out = lax.all_to_all(send_grad, "ep", 0, 1).reshape(local_exp, ep_size * capacity, width)
    g_w_down = jnp.einsum("erf,erd->efd", hidden, grad_exp_out, preferred_element_type=jnp.float32)
    grad_hidden = jnp.einsum("erd,efd->erf", grad_exp_out, w_down, preferred_element_type=jnp.float32)
    grad_a_one = (grad_hidden * a_three * silu_grad(a_one)).astype(jnp.bfloat16)
    grad_a_three = (grad_hidden * jax.nn.silu(a_one)).astype(jnp.bfloat16)
    g_w_gate = jnp.einsum("erd,erf->edf", recv_rows, grad_a_one, preferred_element_type=jnp.float32)
    g_w_up = jnp.einsum("erd,erf->edf", recv_rows, grad_a_three, preferred_element_type=jnp.float32)
    grad_rows = (jnp.einsum("erf,edf->erd", grad_a_one, w_gate, preferred_element_type=jnp.float32) + jnp.einsum("erf,edf->erd", grad_a_three, w_up, preferred_element_type=jnp.float32)).astype(jnp.bfloat16)
    grad_back = lax.all_to_all(grad_rows.reshape(local_exp, ep_size, capacity, width), "ep", 1, 0).reshape(local_exp * ep_size * capacity, width)
    grad_routed = jnp.sum(jnp.take(grad_back, slot_flat, axis=0).reshape(tokens, top, width).astype(jnp.float32), axis=1)
    g_ws_down = contract_rows(shared_hidden, grad_y)
    grad_shared = contract_cols(grad_y, ws_down)
    grad_s_one = (grad_shared * s_three * silu_grad(s_one)).astype(jnp.bfloat16)
    grad_s_three = (grad_shared * jax.nn.silu(s_one)).astype(jnp.bfloat16)
    g_ws_gate = contract_rows(mixed, grad_s_one)
    g_ws_up = contract_rows(mixed, grad_s_three)
    grad_mixed = (grad_y32 + grad_routed + contract_cols(grad_s_one, ws_gate) + contract_cols(grad_s_three, ws_up)).astype(jnp.bfloat16)
    g_w_dense = contract_rows(act, grad_mixed)
    grad_act = (grad_mixed.astype(jnp.float32) + contract_cols(grad_mixed, w_dense)).astype(jnp.bfloat16)
    dense_grads = (g_w_dense.astype(jnp.bfloat16), g_ws_gate.astype(jnp.bfloat16), g_ws_up.astype(jnp.bfloat16), g_ws_down.astype(jnp.bfloat16))
    expert_grads = (g_w_gate.astype(jnp.bfloat16), g_w_up.astype(jnp.bfloat16), g_w_down.astype(jnp.bfloat16))
    return grad_act, dense_grads, expert_grads


def solution(mesh):
    ep_size = mesh.shape["ep"]
    tok_spec = P(ALL_AXES, None)
    route_spec = P(None, ALL_AXES, None)
    exp_spec = P(None, "ep", None, None)
    repl_spec = P(None, None, None)

    def body(act_in, grad_out, slot_ids, gate_vals, w_dense, w_gate, w_up, w_down, ws_gate, ws_up, ws_down):
        layers = w_dense.shape[0]
        all_weights = [(w_dense[layer], w_gate[layer], w_up[layer], w_down[layer], ws_gate[layer], ws_up[layer], ws_down[layer]) for layer in range(layers)]
        saved_all = []
        act = act_in
        for layer in range(layers):
            saved = layer_front(act, all_weights[layer], slot_ids[layer], ep_size)
            saved_all.append(saved)
            if layer + 1 < layers:
                act = layer_finish(saved, all_weights[layer], gate_vals[layer], ep_size)
        grad_act = grad_out
        dense_sums = [None] * layers
        expert_sums = [None] * layers
        for layer in reversed(range(layers)):
            grad_act, dense_grads, expert_grads = layer_backward(grad_act, saved_all[layer], all_weights[layer], gate_vals[layer], ep_size)
            dense_sums[layer] = [lax.psum(part, ALL_AXES) for part in dense_grads]
            expert_sums[layer] = [lax.psum(part, "dp") for part in expert_grads]
        dense_out = [jnp.stack([dense_sums[layer][which] for layer in range(layers)]) for which in range(4)]
        expert_out = [jnp.stack([expert_sums[layer][which] for layer in range(layers)]) for which in range(3)]
        return (grad_act, dense_out[0], expert_out[0], expert_out[1], expert_out[2], dense_out[1], dense_out[2], dense_out[3])

    return jax.shard_map(body, mesh=mesh, in_specs=(tok_spec, tok_spec, route_spec, route_spec, repl_spec, exp_spec, exp_spec, exp_spec, repl_spec, repl_spec, repl_spec), out_specs=(tok_spec, repl_spec, exp_spec, exp_spec, exp_spec, repl_spec, repl_spec, repl_spec), check_vma=False)
```

profile of v0, /device:TPU:0, one launch (start us, length us, event | category | flops | bytes accessed | tf_op | source)
XLA Modules:
  0.0 6173.3 jit_solution(7574112656867575531)
XLA Ops:
  9.1 60.4 scatter_custom_fusion.1
  80.2 132.0 %gather_fusion.1 = bf16[32768,448]{1,0:T(8,128)(2,1)} fusion(bf16[2049,448]{1,0:T(8,128)(2,1)S(1)} %concatenate.13.clone, s32[32768]{0:T(1024)S(1)} %get-tuple-element.60), kind=kCustom, calls=%fused_computation.1.clone | custom fusion | bytes 58851328 | tf_op jit(solution)/shard_map/jit(_take)/gather | solution.py:35
  212.1 22.9 broadcast_select_fusion.2
  235.0 39.8 copy.63
  288.9 317.2 %all-to-all-done.1 = bf16[2,32,1,512,448]{3,4,1,2,0:T(8,128)(2,1)} async-done(((bf16[2,32,1,512,448]{3,4,1,2,0:T(8,128)(2,1)}), bf16[2,32,1,512,448]{3,4,1,2,0:T(8,128)(2,1)}, u32[]{:S(2)}, u32[]{:S(2)}) %all-to-all-start.1) | async-done | bytes 29360160 | tf_op jit(solution)/shard_map/all_to_all | solution.py:36
  606.1 53.3 copy.64
  659.4 47.1 reshape_squeeze.34
  706.5 29.4 fusion.24
  735.9 45.3 multiply_convert_fusion.5
  781.2 26.6 convolution_convert_fusion
  807.8 47.7 broadcast_in_dim_reshape.23
  855.4 20.4 copy.65
  889.5 60.6 scatter_custom_fusion
  971.3 140.9 %gather_fusion = bf16[32768,448]{1,0:T(8,128)(2,1)} fusion(bf16[16385,448]{1,0:T(8,128)(2,1)} %concatenate.12, s32[32768]{0:T(1024)S(1)} %get-tuple-element.66), kind=kCustom, calls=%fused_computation.clone | custom fusion | bytes 58851328 | tf_op jit(solution)/shard_map/jit(_take)/gather | solution.py:72
  1125.1 19.6 multiply_convert_fusion.12
  1144.7 60.6 all-to-all-done.2
  1205.4 40.5 copy.66
  1245.9 266.4 %gather_fusion.2 = bf16[16384,448]{1,0:T(8,128)(2,1)} fusion(bf16[32768,448]{1,0:T(8,128)(2,1)} %bitcast.244, s32[16384]{0:T(1024)S(1)} %fusion.98), kind=kCustom, calls=%fused_computation.2.clone | custom fusion | bytes 29425664 | tf_op jit(solution)/shard_map/jit(_take)/gather | solution.py:56
  1512.3 29.0 fusion.2
  1565.5 131.9 %gather_fusion.3 = bf16[32768,448]{1,0:T(8,128)(2,1)} fusion(bf16[2049,448]{1,0:T(8,128)(2,1)S(1)} %concatenate.14.clone, s32[32768]{0:T(1024)S(1)} %copy-done.23), kind=kCustom, calls=%fused_computation.4.clone | custom fusion | bytes 58851328 | tf_op jit(solution)/shard_map/jit(_take)/gather | solution.py:35
  1697.5 43.5 broadcast_select_fusion.1
  1741.0 39.4 copy.69
  1792.7 39.4 copy.57
  1832.1 276.4 %all-to-all-done.3 = bf16[2,32,1,512,448]{3,4,1,2,0:T(8,128)(2,1)} async-done(((bf16[2,32,1,512,448]{3,4,1,2,0:T(8,128)(2,1)}), bf16[2,32,1,512,448]{3,4,1,2,0:T(8,128)(2,1)}, u32[]{:S(2)}, u32[]{:S(2)}) %all-to-all-start.3) | async-done | bytes 29360160 | tf_op jit(solution)/shard_map/all_to_all | solution.py:36
  2121.1 53.3 copy.70
  2174.4 47.1 reshape_squeeze.37
  2221.5 29.5 fusion.14
  2250.9 29.4 fusion.11
  2280.3 155.8 %all-to-all-done = bf16[2,32,1,512,448]{3,4,1,2,0:T(8,128)(2,1)} async-done(((bf16[2,32,1,512,448]{3,4,1,2,0:T(8,128)(2,1)}), bf16[2,32,1,512,448]{3,4,1,2,0:T(8,128)(2,1)}, u32[]{:S(2)}, u32[]{:S(2)}) %all-to-all-start) | async-done | bytes 29360160 | tf_op jit(solution)/shard_map/all_to_all | solution.py:73
  2436.1 53.3 copy.58
  2489.3 47.1 reshape_squeeze.32
  2536.4 53.4 multiply_convert_fusion.3
  2589.8 33.5 fusion.9
  2623.3 40.6 add_convert_fusion.1
  2663.9 47.7 broadcast_in_dim_reshape.25
  2711.6 20.4 copy.71
  2770.6 24.9 multiply_convert_fusion.10
  2812.7 246.2 %all-to-all-done.4 = bf16[1,32,2,512,448]{3,4,1,0,2:T(8,128)(2,1)} async-done(((bf16[1,32,2,512,448]{3,4,1,0,2:T(8,128)(2,1)}), bf16[1,32,2,512,448]{3,4,1,0,2:T(8,128)(2,1)}, u32[]{:S(2)}, u32[]{:S(2)}) %all-to-all-start.4) | async-done | bytes 29360160 | tf_op jit(solution)/shard_map/all_to_all | solution.py:81
  3059.0 40.3 copy.72
  3099.3 266.2 %gather_fusion.4 = bf16[16384,448]{1,0:T(8,128)(2,1)} fusion(bf16[32768,448]{1,0:T(8,128)(2,1)} %bitcast.242, s32[16384]{0:T(1024)S(1)} %fusion.99), kind=kCustom, calls=%fused_computation.5.clone | custom fusion | bytes 29425664 | tf_op jit(solution)/shard_map/jit(_take)/gather | solution.py:82
  3419.9 140.7 %gather_fusion.5 = bf16[32768,448]{1,0:T(8,128)(2,1)} fusion(bf16[16385,448]{1,0:T(8,128)(2,1)} %concatenate.15, s32[32768]{0:T(1024)S(1)} %copy-done.22), kind=kCustom, calls=%fused_computation.3.clone | custom fusion | bytes 58851328 | tf_op jit(solution)/shard_map/jit(_take)/gather | solution.py:72
  3560.6 22.9 broadcast_select_fusion
  3583.5 39.3 copy.76
  3664.2 22.0 convert_bitcast_fusion.2
  3686.3 40.8 convert_bitcast_fusion
  3727.1 221.6 %all-to-all-done.5 = bf16[2,32,1,512,448]{3,4,1,2,0:T(8,128)(2,1)} async-done(((bf16[2,32,1,512,448]{3,4,1,2,0:T(8,128)(2,1)}), bf16[2,32,1,512,448]{3,4,1,2,0:T(8,128)(2,1)}, u32[]{:S(2)}, u32[]{:S(2)}) %all-to-all-start.5) | async-done | bytes 29360160 | tf_op jit(solution)/shard_map/all_to_all | solution.py:73
  3948.7 53.3 copy.77
  4001.9 47.1 reshape_squeeze.40
  4049.0 53.6 multiply_convert_fusion.1
  4102.6 33.1 fusion.22
  4135.7 40.5 add_convert_fusion
  4176.2 47.7 broadcast_in_dim_reshape.27
  4223.9 20.4 copy.78
  4256.8 22.7 convert_bitcast_fusion.4
  4293.7 25.0 multiply_convert_fusion.8
  4342.2 227.2 %all-to-all-done.6 = bf16[1,32,2,512,448]{3,4,1,0,2:T(8,128)(2,1)} async-done(((bf16[1,32,2,512,448]{3,4,1,0,2:T(8,128)(2,1)}), bf16[1,32,2,512,448]{3,4,1,0,2:T(8,128)(2,1)}, u32[]{:S(2)}, u32[]{:S(2)}) %all-to-all-start.6) | async-done | bytes 29360160 | tf_op jit(solution)/shard_map/all_to_all | solution.py:81
  4569.4 40.3 copy.79
  4609.8 266.6 %gather_fusion.6 = bf16[16384,448]{1,0:T(8,128)(2,1)} fusion(bf16[32768,448]{1,0:T(8,128)(2,1)} %bitcast.243, s32[16384]{0:T(1024)S(1)} %copy-done.21), kind=kCustom, calls=%fused_computation.6.clone | custom fusion | bytes 29425664 | tf_op jit(solution)/shard_map/jit(_take)/gather | solution.py:82
  4913.1 24.3 convert_bitcast_fusion.1
  4937.4 22.2 convert_bitcast_fusion.3
  4959.6 22.1 convert_bitcast_fusion.5
  4985.8 109.8 %all-reduce.9.cloned.1.call-done = (bf16[1,448,448]{1,2,0:T(8,128)(2,1)}, bf16[1,448,448]{1,2,0:T(8,128)(2,1)}, bf16[1,448,2560]{2,1,0:T(8,128)(2,1)}, bf16[1,44...) async-done(((bf16[1,448,448]{1,2,0:T(8,128)(2,1)}, ...) | async-done | bytes 14565392 | tf_op jit(solution)/shard_map/psum | solution.py:119
  5110.7 1012.8 %all-reduce.11.cloned.1.call-done = (bf16[1,32,448,320]{2,3,1,0:T(8,128)(2,1)}, bf16[1,32,448,320]{2,3,1,0:T(8,128)(2,1)}, bf16[1,32,448,320]{2,3,1,0:T(8,128)(2...) async-done(((bf16[1,32,448,320]{2,3,1,0:T(8,128)(2,1)}, bf16[1,32,448,320]{2,3,1,0:T(8,128)(2,1)}, ...) | async-done | bytes 55050256 | tf_op jit(solution)/shard_map/psum | solution.py:120
  6123.5 21.0 pad_maximum_fusion
  (199 shorter events, 402.8 us)
Async XLA Ops:
  7.2 63.0 %copy-start.33 = (s32[16384]{0:T(1024)}, s32[16384]{0:T(1024)S(1)}, u32[]{:S(2)}) copy-start(s32[16384]{0:T(1024)S(1)} %iota_add_fusion) | copy-start | bytes 196612
  8.4 65.9 %copy-start.4 = (s32[1,2048,8]{2,1,0:T(8,128)}, s32[1,2048,8]{2,1,0:T(8,128)S(1)}, u32[]{:S(2)}) copy-start(s32[1,2048,8]{2,1,0:T(8,128)S(1)} %copy.60) | copy-start | bytes 196612
  74.4 1.2 copy-start.12
  274.8 331.3 %all-to-all-start.1 = ((bf16[2,32,1,512,448]{3,4,1,2,0:T(8,128)(2,1)}), bf16[2,32,1,512,448]{3,4,1,2,0:T(8,128)(2,1)}, u32[]{:S(2)}, u32[]{:S(2)}) async-start(bf16[2,32,1,512,448]{3,4,1,2,0:T(8,128)(2,1)} %copy.63), calls=%async_computation.1 | async-start | bytes 58720256 | tf_op jit(solution)/shard_map/all_to_all | solution.py:36
  287.8 371.6 %copy-start.2 = (s32[1,2048,8]{2,1,0:T(8,128)}, s32[1,2048,8]{2,1,0:T(8,128)S(1)}, u32[]{:S(2)}) copy-start(s32[1,2048,8]{2,1,0:T(8,128)S(1)} %copy.53) | copy-start | bytes 196612
  875.8 13.1 copy-start.26
  875.8 13.1 copy-start.5
  875.8 74.2 %copy-start.30 = (f32[2,2048,8]{1,2,0:T(8,128)S(1)}, f32[2,2048,8]{1,2,0:T(8,128)}, u32[]{:S(2)}) copy-start(f32[2,2048,8]{1,2,0:T(8,128)} %param.20) | copy-start | bytes 393220
  875.8 77.0 %copy-start.9 = (bf16[2048,448]{0,1:T(8,128)(2,1)S(1)}, bf16[2048,448]{0,1:T(8,128)(2,1)}, u32[]{:S(2)}) copy-start(bf16[2048,448]{0,1:T(8,128)(2,1)} %param.18) | copy-start | bytes 5505028
  875.8 329.5 %all-to-all-start.2 = ((bf16[1,32,2,512,448]{3,4,1,0,2:T(8,128)(2,1)}), bf16[1,32,2,512,448]{3,4,1,0,2:T(8,128)(2,1)}, u32[]{:S(2)}, u32[]{:S(2)}) async-start(bf16[1,32,2,512,448]{3,4,1,0,2:T(8,128)(2,1)} %copy.65), calls=%async_computation.2 | async-start | bytes 58720256 | tf_op jit(solution)/shard_map/all_to_all | solution.py:55
  971.3 141.7 %copy-start.13 = (bf16[2048,448]{0,1:T(8,128)(2,1)S(1)}, bf16[2048,448]{0,1:T(8,128)(2,1)}, u32[]{:S(2)}) copy-start(bf16[2048,448]{0,1:T(8,128)(2,1)} %copy-done.12) | copy-start | bytes 5505028
  1112.2 400.1 %copy-start.27 = (pred[16384]{0:T(1024)(128)(4,1)}, pred[16384]{0:T(1024)(128)(4,1)S(1)}, u32[]{:S(2)}) copy-start(pred[16384]{0:T(1024)(128)(4,1)S(1)} %compare_and_fusion.5) | copy-start | bytes 49156
  1112.2 133.6 %copy-start.20 = (s32[16384]{0:T(1024)}, s32[16384]{0:T(1024)S(1)}, u32[]{:S(2)}) copy-start(s32[16384]{0:T(1024)S(1)} %fusion.98) | copy-start | bytes 196612
  1245.9 266.4 %copy-start.6 = (f32[2048,8]{1,0:T(8,128)S(1)}, f32[2048,8]{1,0:T(8,128)}, u32[]{:S(2)}) copy-start(f32[2048,8]{1,0:T(8,128)} %copy.59) | copy-start | bytes 196612
  1546.5 12.0 copy-start.35
  1558.5 7.0 copy-start.23
  1559.7 1.3 copy-start.15
  1565.5 132.0 %copy-start.31 = (pred[32768]{0:T(1024)(128)(4,1)S(1)}, pred[32768]{0:T(1024)(128)(4,1)}, u32[]{:S(2)}) copy-start(pred[32768]{0:T(1024)(128)(4,1)} %get-tuple-element.64) | copy-start | bytes 98308
  1565.5 132.0 %copy-start.32 = (pred[32768]{0:T(1024)(128)(4,1)S(1)}, pred[32768]{0:T(1024)(128)(4,1)}, u32[]{:S(2)}) copy-start(pred[32768]{0:T(1024)(128)(4,1)} %get-tuple-element.65) | copy-start | bytes 98308
  1780.4 328.1 %all-to-all-start.3 = ((bf16[2,32,1,512,448]{3,4,1,2,0:T(8,128)(2,1)}), bf16[2,32,1,512,448]{3,4,1,2,0:T(8,128)(2,1)}, u32[]{:S(2)}, u32[]{:S(2)}) async-start(bf16[2,32,1,512,448]{3,4,1,2,0:T(8,128)(2,1)} %copy.69), calls=%async_computation.3 | async-start | bytes 58720256 | tf_op jit(solution)/shard_map/all_to_all | solution.py:36
  2108.5 327.6 %all-to-all-start = ((bf16[2,32,1,512,448]{3,4,1,2,0:T(8,128)(2,1)}), bf16[2,32,1,512,448]{3,4,1,2,0:T(8,128)(2,1)}, u32[]{:S(2)}, u32[]{:S(2)}) async-start(bf16[2,32,1,512,448]{3,4,1,2,0:T(8,128)(2,1)} %copy.57), calls=%async_computation | async-start | bytes 58720256 | tf_op jit(solution)/shard_map/all_to_all | solution.py:73
  2732.0 12.7 copy-start.3
  2732.0 13.2 copy-start.25
  2732.0 14.7 copy-start.16
  2732.1 326.9 %all-to-all-start.4 = ((bf16[1,32,2,512,448]{3,4,1,0,2:T(8,128)(2,1)}), bf16[1,32,2,512,448]{3,4,1,0,2:T(8,128)(2,1)}, u32[]{:S(2)}, u32[]{:S(2)}) async-start(bf16[1,32,2,512,448]{3,4,1,0,2:T(8,128)(2,1)} %copy.71), calls=%async_computation.4 | async-start | bytes 58720256 | tf_op jit(solution)/shard_map/all_to_all | solution.py:81
  2746.7 12.0 copy-start.17
  2746.7 23.8 slice-start.6
  2758.7 11.8 copy-start.10
  2758.7 11.8 slice-start.7
  2758.7 47.2 slice-start.10
  2770.5 35.3 slice-start.11
  2795.4 10.5 copy-start.42
  3387.1 13.1 copy-start.36
  3399.0 1.2 copy-start.39
  3400.3 4.1 copy-start.24
  3401.4 18.4 copy-start.18
  3410.4 9.4 copy-start.22
  3419.8 140.8 %copy-start.29 = (pred[32768]{0:T(1024)(128)(4,1)S(1)}, pred[32768]{0:T(1024)(128)(4,1)}, u32[]{:S(2)}) copy-start(pred[32768]{0:T(1024)(128)(4,1)} %get-tuple-element.57) | copy-start | bytes 98308
  3622.8 325.9 %all-to-all-start.5 = ((bf16[2,32,1,512,448]{3,4,1,2,0:T(8,128)(2,1)}), bf16[2,32,1,512,448]{3,4,1,2,0:T(8,128)(2,1)}, u32[]{:S(2)}, u32[]{:S(2)}) async-start(bf16[2,32,1,512,448]{3,4,1,2,0:T(8,128)(2,1)} %copy.76), calls=%async_computation.5 | async-start | bytes 58720256 | tf_op jit(solution)/shard_map/all_to_all | solution.py:73
  3635.2 10.9 copy-start.11
  4244.3 325.2 %all-to-all-start.6 = ((bf16[1,32,2,512,448]{3,4,1,0,2:T(8,128)(2,1)}), bf16[1,32,2,512,448]{3,4,1,0,2:T(8,128)(2,1)}, u32[]{:S(2)}, u32[]{:S(2)}) async-start(bf16[1,32,2,512,448]{3,4,1,0,2:T(8,128)(2,1)} %copy.78), calls=%async_computation.6 | async-start | bytes 58720256 | tf_op jit(solution)/shard_map/all_to_all | solution.py:81
  4256.7 26.9 copy-start.19
  4256.7 838.8 %all-reduce.9.cloned.1.call-start = ((), (), s32[]{:S(2)}) async-start(), calls=%async_computation.7 | async-start | bytes 29360128 | tf_op jit(solution)/shard_map/psum | solution.py:119
  4279.5 14.3 slice-start.8
  4283.6 10.2 slice-start.9
  4293.7 25.0 copy-start.14
  4318.7 10.3 copy-start.43
  4318.7 16.7 slice-start.12
  4329.0 6.4 slice-start.13
  4569.4 40.4 copy-start.21
  4609.8 266.6 %copy-start.28 = (pred[16384]{0:T(1024)(128)(4,1)S(1)}, pred[16384]{0:T(1024)(128)(4,1)}, u32[]{:S(2)}) copy-start(pred[16384]{0:T(1024)(128)(4,1)} %copy-done.27) | copy-start | bytes 49156
  4898.1 13.1 copy-start.34
  4913.0 1210.5 %all-reduce.11.cloned.1.call-start = ((), (), s32[]{:S(2)}) async-start(), calls=%async_computation.8 | async-start | bytes 125829120 | tf_op jit(solution)/shard_map/psum | solution.py:120
  4981.6 1.8 copy-start.41
  5095.5 12.6 copy-start.7
  5098.2 10.0 copy-start.8
  6123.5 21.0 copy-start
  6123.5 21.0 copy-start.1
  6123.5 31.4 slice-start
  6123.5 31.4 slice-start.1
  6123.5 31.4 slice-start.3
  6123.5 32.7 slice-start.4
  6144.5 12.5 slice-start.2
  6144.5 13.1 slice-start.5
  (3 other events, 3.6 us)
Sparse Core Ops, SparseCore 0:
  4913.2 182.3 all-reduce.8
  5099.2 1024.2 all-reduce.10
where the time goes:
time: 6210 us; the launch traced here: 6170 us
  waiting for transfers between devices  2630 us (42%)
  local copies, waits for them, and re-layouts  2420 us (39%)
  matrix products  802 us (13%)
  other arithmetic  220 us (4%)
  starting transfers between devices  88 us (1%)
    psum x1, waiting for transfers between devices, body(): expert_sums[layer] = [lax.psum(part, 'dp') for part in expert_grads]  1010 us
    all_to_all x2, waiting for transfers between devices, layer_front(): lax.all_to_all(send_buf, 'ep', 0, 1)  594 us
    gather x2, local copies, waits for them, and re-layouts, layer_backward(): jnp.take(grad_back, slot_flat, axis=0).reshape(tokens, top, width)  533 us
    all_to_all x2, waiting for transfers between devices, layer_backward(): lax.all_to_all(grad_rows.reshape(local_exp, ep_size, capacity, width), 'e...  473 us
    all_to_all x2, waiting for transfers between devices, layer_backward(): lax.all_to_all(send_grad, 'ep', 0, 1)  377 us
    gather x2, local copies, waits for them, and re-layouts, layer_backward(): jnp.take(grad_ext, slot_owner, axis=0)  282 us
    gather x1, local copies, waits for them, and re-layouts, layer_finish(): picked = jnp.take(back_rows, slot_flat, axis=0).reshape(tokens, top, width)  266 us
    gather x2, local copies, waits for them, and re-layouts, layer_front(): jnp.take(mixed_ext, tok_owner, axis=0)  264 us
  transfers between devices with their start and end apart: 9, of which 9 were waited for; matrix products, arithmetic and copies ran while one was open for 13% of the time, Pallas kernels for 0%

commit v1 on v0

v1 whole, which is shorter than its diff:
```python
import functools
import jax
import jax.numpy as jnp
from jax import lax
from jax.experimental import pallas as pl
from jax.experimental.pallas import tpu as pltpu
from jax.sharding import PartitionSpec as P

ALL_AXES = ("ep", "dp")
F32 = jnp.float32
BF16 = jnp.bfloat16
TILE = 256
VMEM_MAX = 60 * 1024 * 1024


def dot(left, right, dims=((1,), (0,))):
    return lax.dot_general(left, right, (dims, ((), ())), preferred_element_type=F32)


def silu_grad(pre_act):
    sigma = jax.nn.sigmoid(pre_act)
    return sigma * (1.0 + pre_act * (1.0 - sigma))


def contract_rows(left, right):
    return dot(left, right, ((0,), (0,)))


def contract_cols(left, right):
    return dot(left, right, ((1,), (1,)))


def route_kernel(exp_ref, gate_ref, pos_ref, gmat_ref, cnt_ref):
    sources, top, tokens = exp_ref.shape
    local_exp = pos_ref.shape[1]
    block = 256
    upper = (lax.broadcasted_iota(jnp.int32, (block, block), 0) < lax.broadcasted_iota(jnp.int32, (block, block), 1)).astype(BF16)
    exp_iota = lax.broadcasted_iota(jnp.int32, (local_exp, block), 0)
    for src in range(sources):
        carry = jnp.zeros((local_exp, 1), F32)
        for start in range(0, tokens, block):
            member = jnp.zeros((local_exp, block), F32)
            gates = jnp.zeros((local_exp, block), F32)
            for j in range(top):
                hit = exp_ref[src, j:j + 1, start:start + block] == exp_iota
                member = member + jnp.where(hit, 1.0, 0.0)
                gates = gates + jnp.where(hit, gate_ref[src, j:j + 1, start:start + block], 0.0)
            before = dot(member.astype(BF16), upper) + carry
            pos_ref[src, :, start:start + block] = jnp.where(member > 0.0, before, -1.0).astype(jnp.int32)
            gmat_ref[src, :, start:start + block] = gates
            carry = carry + jnp.sum(member, axis=1, keepdims=True)
        cnt_ref[src] = jnp.broadcast_to(carry, cnt_ref.shape[1:]).astype(jnp.int32)


def route(exp_ids, gates, local_exp):
    sources, top, tokens = exp_ids.shape
    pos, gmat, cnt = pl.pallas_call(
        route_kernel,
        out_shape=(
            jax.ShapeDtypeStruct((sources, local_exp, tokens), jnp.int32),
            jax.ShapeDtypeStruct((sources, local_exp, tokens), F32),
            jax.ShapeDtypeStruct((sources, local_exp, 128), jnp.int32),
        ),
        cost_estimate=pl.CostEstimate(flops=2 * sources * local_exp * tokens * 256, bytes_accessed=4 * sources * local_exp * tokens * 2, transcendentals=0),
        name="route",
    )(exp_ids, gates)
    return pos, gmat, cnt[:, :, 0]


def pick_rows(pos_ref, src, exp, row0):
    pos = pos_ref[src, pl.ds(exp, 1), :]
    hit = pos == row0 + lax.broadcasted_iota(jnp.int32, (TILE, pos.shape[1]), 0)
    return jnp.where(hit, 1.0, 0.0).astype(BF16)


def row_tiles(cnt_ref, exp):
    tiles0 = (cnt_ref[0, exp] + TILE - 1) // TILE
    return tiles0, tiles0 + (cnt_ref[1, exp] + TILE - 1) // TILE


def forward_kernel(cnt_ref, pos_ref, gmat_ref, tok_ref, wg_ref, wu_ref, wd_ref, out_ref):
    exp = pl.program_id(0)

    @pl.when(exp == 0)
    def _():
        out_ref[...] = jnp.zeros_like(out_ref)

    tiles0, tiles = row_tiles(cnt_ref, exp)

    def step(q, _):
        src = (q >= tiles0).astype(jnp.int32)
        pick = pick_rows(pos_ref, src, exp, (q - src * tiles0) * TILE)
        rows = contract_cols(tok_ref[src], pick).astype(BF16)
        a_one = dot(wg_ref[0, 0], rows)
        a_three = dot(wu_ref[0, 0], rows)
        hidden = (a_one * jax.nn.sigmoid(a_one) * a_three).astype(BF16)
        o_rows = contract_rows(wd_ref[0, 0], hidden).astype(BF16)
        out_ref[src] += gmat_ref[src, pl.ds(exp, 1), :] * dot(o_rows, pick)
        return 0

    lax.fori_loop(0, tiles, step, 0)


def whole_spec(*shape):
    return pl.BlockSpec(shape, lambda e, c: (0,) * len(shape), pipeline_mode=pl.Buffered(1))


def layer_spec(layer, inner, width):
    return pl.BlockSpec((1, 1, inner, width), lambda e, c: (layer, e, 0, 0))


def expert_forward(layer, cnt, pos, gmat, tok, w_gate, w_up, w_down):
    sources, width, tokens = tok.shape
    _, local_exp, inner, _ = w_gate.shape
    rows = sources * tokens * 4
    return pl.pallas_call(
        forward_kernel,
        out_shape=jax.ShapeDtypeStruct((sources, width, tokens), F32),
        grid_spec=pltpu.PrefetchScalarGridSpec(
            num_scalar_prefetch=1,
            grid=(local_exp,),
            in_specs=[whole_spec(*pos.shape), whole_spec(*gmat.shape), whole_spec(*tok.shape)] + [layer_spec(layer, inner, width)] * 3,
            out_specs=whole_spec(sources, width, tokens),
        ),
        compiler_params=pltpu.CompilerParams(dimension_semantics=("arbitrary",), vmem_limit_bytes=VMEM_MAX),
        cost_estimate=pl.CostEstimate(flops=rows * width * (4 * tokens + 6 * inner), bytes_accessed=6 * local_exp * width * inner, transcendentals=rows * inner),
        name="expert_forward",
    )(cnt, pos, gmat, tok, w_gate, w_up, w_down)


def pack_rows(inner, width):
    full = width // 128
    return 3 * inner * full + 3 * inner * (width - full * 128) // 128


def backward_kernel(cnt_ref, pos_ref, gmat_ref, tok_ref, gy_ref, wg_ref, wu_ref, wd_ref, own_ref, peer_ref, pack_ref, acc_ref, wacc_ref):
    exp = pl.program_id(0)
    _, width, tokens = tok_ref.shape
    inner = wg_ref.shape[2]

    @pl.when(exp == 0)
    def _():
        acc_ref[...] = jnp.zeros_like(acc_ref)

    wacc_ref[...] = jnp.zeros_like(wacc_ref)
    tiles0, tiles = row_tiles(cnt_ref, exp)

    def step(q, _):
        src = (q >= tiles0).astype(jnp.int32)
        pick = pick_rows(pos_ref, src, exp, (q - src * tiles0) * TILE)
        gate = gmat_ref[src, pl.ds(exp, 1), :]
        high = gate.astype(BF16).astype(F32)
        mid = (gate - high).astype(BF16).astype(F32)
        low = gate - high - mid
        part = lax.broadcasted_iota(jnp.int32, (16, tokens), 0)
        gate_parts = jnp.where(part == 0, high, jnp.where(part == 1, mid, jnp.where(part == 2, low, 0.0))).astype(BF16)
        table = jnp.concatenate([tok_ref[src], gy_ref[src], gate_parts], axis=0)
        got = contract_cols(table, pick)
        rows = got[:width].astype(BF16)
        row_gate = jnp.sum(got[2 * width:], axis=0, keepdims=True)
        g_rows = (row_gate * got[width:2 * width]).astype(BF16)
        a_one = dot(wg_ref[0, 0], rows)
        a_three = dot(wu_ref[0, 0], rows)
        g_hidden = dot(wd_ref[0, 0], g_rows)
        sigma = jax.nn.sigmoid(a_one)
        silu = a_one * sigma
        hidden = (silu * a_three).astype(BF16)
        g_one = (g_hidden * a_three * (sigma * (1.0 + a_one * (1.0 - sigma)))).astype(BF16)
        g_three = (g_hidden * silu).astype(BF16)
        wacc_ref[:inner] += contract_cols(g_one, rows)
        wacc_ref[inner:2 * inner] += contract_cols(g_three, rows)
        wacc_ref[2 * inner:] += contract_cols(hidden, g_rows)
        g_x = (contract_rows(wg_ref[0, 0], g_one) + contract_rows(wu_ref[0, 0], g_three)).astype(BF16)
        acc_ref[src] += dot(g_x, pick)
        return 0

    lax.fori_loop(0, tiles, step, 0)
    full = width // 128
    size = 3 * inner
    for lane in range(full):
        pack_ref[0, lane * size:(lane + 1) * size, :] = wacc_ref[:, lane * 128:(lane + 1) * 128].astype(BF16)
    rest = wacc_ref[:, full * 128:].astype(BF16)
    pack_ref[0, full * size:, :] = jnp.concatenate([rest[:size // 2], rest[size // 2:]], axis=1)

    @pl.when(exp == pl.num_programs(0) - 1)
    def _():
        own_ref[...] = acc_ref[0]
        peer_ref[...] = acc_ref[1].astype(BF16)


def expert_backward(layer, cnt, pos, gmat, tok, gy, w_gate, w_up, w_down):
    sources, width, tokens = tok.shape
    _, local_exp, inner, _ = w_gate.shape
    rows = sources * tokens * 4
    packed = pack_rows(inner, width)
    return pl.pallas_call(
        backward_kernel,
        out_shape=(
            jax.ShapeDtypeStruct((width, tokens), F32),
            jax.ShapeDtypeStruct((width, tokens), BF16),
            jax.ShapeDtypeStruct((local_exp, packed, 128), BF16),
        ),
        grid_spec=pltpu.PrefetchScalarGridSpec(
            num_scalar_prefetch=1,
            grid=(local_exp,),
            in_specs=[whole_spec(*pos.shape), whole_spec(*gmat.shape), whole_spec(*tok.shape), whole_spec(*gy.shape)] + [layer_spec(layer, inner, width)] * 3,
            out_specs=[whole_spec(width, tokens), whole_spec(width, tokens), pl.BlockSpec((1, packed, 128), lambda e, c: (e, 0, 0))],
            scratch_shapes=[pltpu.VMEM((sources, width, tokens), F32), pltpu.VMEM((3 * inner, width), F32)],
        ),
        compiler_params=pltpu.CompilerParams(dimension_semantics=("arbitrary",), vmem_limit_bytes=VMEM_MAX),
        cost_estimate=pl.CostEstimate(flops=rows * width * (6 * tokens + 18 * inner), bytes_accessed=12 * local_exp * width * inner, transcendentals=rows * inner),
        name="expert_backward",
    )(cnt, pos, gmat, tok, gy, w_gate, w_up, w_down)


def unpack_kernel(place_ref, pack_ref, *refs):
    outs = refs[len(refs) // 2:]
    inner, width = outs[0].shape[2:]
    full = width // 128
    size = 3 * inner
    half = size // 2
    for which, out in enumerate(outs):
        first = which * inner
        for lane in range(full):
            out[0, 0, :, lane * 128:(lane + 1) * 128] = pack_ref[0, lane * size + first:lane * size + first + inner, :]
        for start in range(first, first + inner, inner // 2):
            col = (start // half) * 64
            row = full * size + start % half
            out[0, 0, start - first:start - first + inner // 2, full * 128:] = pack_ref[0, row:row + inner // 2, col:col + 64]


def unpack_into(layer, place, piece, outs):
    count = piece.shape[0]
    inner, width = outs[0].shape[2:]
    out_spec = pl.BlockSpec((1, 1, inner, width), lambda e, p: (layer, p[0] * count + e, 0, 0))
    return pl.pallas_call(
        unpack_kernel,
        out_shape=tuple(jax.ShapeDtypeStruct(out.shape, out.dtype) for out in outs),
        grid_spec=pltpu.PrefetchScalarGridSpec(
            num_scalar_prefetch=1,
            grid=(count,),
            in_specs=[pl.BlockSpec((1,) + piece.shape[1:], lambda e, p: (e, 0, 0))] + [pl.BlockSpec(memory_space=pl.ANY)] * len(outs),
            out_specs=[out_spec] * len(outs),
        ),
        input_output_aliases={2 + i: i for i in range(len(outs))},
        compiler_params=pltpu.CompilerParams(dimension_semantics=("arbitrary",)),
        cost_estimate=pl.CostEstimate(flops=4 * piece.size, bytes_accessed=4 * piece.size, transcendentals=0),
        name="unpack",
    )(place.reshape(1), piece, *outs)


def swap(value, axis, size, bit):
    return lax.ppermute(value, axis, [(i, i ^ bit) for i in range(size)])


def reduce_over_dp(part, dp_size):
    index = lax.axis_index("dp")
    bits = [1 << b for b in range(dp_size.bit_length() - 1)]
    for bit in bits:
        half = part.shape[0] // 2
        mine = ((index // bit) % 2) * half
        got = swap(lax.dynamic_slice_in_dim(part, half - mine, half), "dp", dp_size, bit)
        part = (lax.dynamic_slice_in_dim(part, mine, half).astype(F32) + got.astype(F32)).astype(BF16)
    pieces = [(part, index)]
    for bit in reversed(bits):
        pieces = pieces + [(swap(piece, "dp", dp_size, bit), place ^ bit) for piece, place in pieces]
    return pieces, bits


def place_of(place, bits):
    return sum(((place // bit) % 2) << (len(bits) - 1 - order) for order, bit in enumerate(bits))


def solution(mesh):
    ep_size = mesh.shape["ep"]
    dp_size = mesh.shape["dp"]
    tok_spec = P(ALL_AXES, None)
    route_spec = P(None, ALL_AXES, None)
    exp_spec = P(None, "ep", None, None)
    repl_spec = P(None, None, None)

    def body(act_in, grad_out, slot_ids, gate_vals, w_dense, w_gate, w_up, w_down, ws_gate, ws_up, ws_down):
        layers, tokens, top = slot_ids.shape
        local_exp, width, inner = w_gate.shape[1:]
        capacity = 2 * tokens * top // (local_exp * ep_size)
        ep_index = lax.axis_index("ep")
        to_peer = lambda value: swap(value, "ep", ep_size, 1)
        pair = lambda value: jnp.stack([value, to_peer(value)])

        w_gate_t = w_gate.swapaxes(2, 3)
        w_up_t = w_up.swapaxes(2, 3)
        slots = pair(slot_ids.swapaxes(1, 2) // capacity) - ep_index * local_exp
        gates = pair(gate_vals.swapaxes(1, 2))
        routes = [route(slots[:, layer], gates[:, layer], local_exp) for layer in range(layers)]
        grad_y = grad_out.T
        grad2 = pair(grad_y)

        act = act_in.T
        saved = []
        for layer in range(layers):
            mixed = (act.astype(F32) + contract_rows(w_dense[layer], act)).astype(BF16)
            mixed2 = pair(mixed)
            s_one = contract_rows(ws_gate[layer], mixed)
            s_three = contract_rows(ws_up[layer], mixed)
            shared_hidden = (jax.nn.silu(s_one) * s_three).astype(BF16)
            saved.append((act, mixed, mixed2, s_one, s_three, shared_hidden))
            if layer + 1 < layers:
                pos, gmat, cnt = routes[layer]
                out = expert_forward(layer, cnt, pos, gmat, mixed2, w_gate_t, w_up_t, w_down)
                routed = out[0] + to_peer(out[1])
                act = (mixed.astype(F32) + routed + contract_rows(ws_down[layer], shared_hidden)).astype(BF16)

        dense_sums = [None] * layers
        expert_out = [jnp.zeros((layers, local_exp, inner, width), BF16) for _ in range(3)]
        for layer in reversed(range(layers)):
            act, mixed, mixed2, s_one, s_three, shared_hidden = saved[layer]
            pos, gmat, cnt = routes[layer]
            if layer + 1 < layers:
                grad2 = pair(grad_y)
            own, peer, packed = expert_backward(layer, cnt, pos, gmat, mixed2, grad2, w_gate_t, w_up_t, w_down)
            grad_routed = own + to_peer(peer).astype(F32)
            g_ws_down = contract_cols(shared_hidden, grad_y)
            grad_shared = dot(ws_down[layer], grad_y)
            grad_s_one = (grad_shared * s_three * silu_grad(s_one)).astype(BF16)
            grad_s_three = (grad_shared * jax.nn.silu(s_one)).astype(BF16)
            g_ws_gate = contract_cols(mixed, grad_s_one)
            g_ws_up = contract_cols(mixed, grad_s_three)
            grad_mixed = (grad_y.astype(F32) + grad_routed + dot(ws_gate[layer], grad_s_one) + dot(ws_up[layer], grad_s_three)).astype(BF16)
            g_w_dense = contract_cols(act, grad_mixed)
            grad_y = (grad_mixed.astype(F32) + dot(w_dense[layer], grad_mixed)).astype(BF16)
            dense_sums[layer] = [lax.psum(part.astype(BF16), ALL_AXES) for part in (g_w_dense, g_ws_gate, g_ws_up, g_ws_down)]
            pieces, bits = reduce_over_dp(packed, dp_size)
            for piece, place in pieces:
                expert_out = unpack_into(layer, place_of(place, bits), piece, expert_out)
        dense_out = [jnp.stack([dense_sums[layer][which] for layer in range(layers)]) for which in range(4)]
        return (grad_y.T, dense_out[0], expert_out[0].swapaxes(2, 3), expert_out[1].swapaxes(2, 3), expert_out[2], dense_out[1], dense_out[2], dense_out[3])

    return jax.shard_map(body, mesh=mesh, in_specs=(tok_spec, tok_spec, route_spec, route_spec, repl_spec, exp_spec, exp_spec, exp_spec, repl_spec, repl_spec, repl_spec), out_specs=(tok_spec, repl_spec, exp_spec, exp_spec, exp_spec, repl_spec, repl_spec, repl_spec), check_vma=False)
```

time: 6210 us -> 2190 us (0.35)
  local copies, waits for them, and re-layouts: 2420 us -> 74 us
  waiting for transfers between devices: 2630 us -> 741 us
  Pallas kernels: 0 us -> 1010 us
  matrix products: 802 us -> 230 us
  other arithmetic: 220 us -> 76.5 us
    all_to_all x7 -> x0, waiting for transfers between devices: 1510 us -> none  [the longest x2 594 us: layer_front(): lax.all_to_all(send_buf, 'ep', 0, 1)]
    gather x7 -> x0, local copies, waits for them, and re-layouts: 1340 us -> none  [the longest x2 533 us: layer_backward(): jnp.take(grad_back, slot_flat, axis=0).reshape(tokens, top, width)]
    psum x2 -> x1, waiting for transfers between devices: 1120 us -> 0.01 us  [body(): lax.psum(part.astype(BF16), ALL_AXES)]
    pallas_call x0 -> x13, Pallas kernels: none -> 1010 us  [the longest x2 725 us: expert_backward(): pl.pallas_call(backward_kernel, out_shape=(jax.ShapeDtypeStruct((width, t...]
    ppermute x0 -> x19, waiting for transfers between devices: none -> 741 us  [swap(): return lax.ppermute(value, axis, [(i, i ^ bit) for i in range(size)])]
    dot_general x40 -> x23, matrix products: 802 us -> 230 us  [dot(): lax.dot_general(left, right, (dims, ((), ())), preferred_element_type=F32)]
    another operation x18 -> x3, local copies, waits for them, and re-layouts: 553 us -> 22.1 us  [the longest x4 173 us: layer_front(): lax.all_to_all(send_buf, 'ep', 0, 1)]
    all_to_all x7 -> x0, local copies, waits for them, and re-layouts: 334 us -> none  [the longest x2 107 us: layer_front(): lax.all_to_all(send_buf, 'ep', 0, 1)]
  transfers between devices with their start and end apart: 9 -> 20, of which waited for: 9 -> 10; matrix products, arithmetic and copies ran while one was open for 13% -> 16% of each run, Pallas kernels for 0% -> 29%
where the time goes in v1:
time: 2190 us; the launch traced here: 2200 us
  Pallas kernels  1010 us (46%)
  waiting for transfers between devices  741 us (34%)
  matrix products  230 us (11%)
  other arithmetic  76.5 us (3%)
  local copies, waits for them, and re-layouts  74 us (3%)
  starting transfers between devices  55.1 us (3%)
    ppermute x19, waiting for transfers between devices, swap(): return lax.ppermute(value, axis, [(i, i ^ bit) for i in range(size)])  741 us
    pallas_call x2, Pallas kernels, expert_backward(): pl.pallas_call(backward_kernel, out_shape=(jax.ShapeDtypeStruct((width, t...  725 us
    dot_general x23, matrix products, dot(): lax.dot_general(left, right, (dims, ((), ())), preferred_element_type=F32)  230 us
    pallas_call x1, Pallas kernels, expert_forward(): pl.pallas_call(forward_kernel, out_shape=jax.ShapeDtypeStruct((sources, w...  210 us
    pallas_call x8, Pallas kernels, unpack_into(): pl.pallas_call(unpack_kernel, out_shape=tuple((jax.ShapeDtypeStruct(out.s...  67.7 us
    ppermute x19, starting transfers between devices, swap(): return lax.ppermute(value, axis, [(i, i ^ bit) for i in range(size)])  55.1 us
  transfers between devices with their start and end apart: 20, of which 10 were waited for; matrix products, arithmetic and copies ran while one was open for 16% of the time, Pallas kernels for 29%

profile of v1, /device:TPU:0, one launch (start us, length us, event | category | flops | bytes accessed | tf_op | source)
XLA Modules:
  0.0 2200.0 jit_solution(2204026487504037983)
XLA Ops:
  8.2 3.4 collective-permute-start
  11.6 3.5 fusion.39
  17.2 10.5 fusion.61
  33.4 24.7 %collective-permute-done.2 = bf16[448,2048]{1,0:T(8,128)(2,1)} collective-permute-done((bf16[448,2048]{1,0:T(8,128)(2,1)S(1)}, bf16[448,2048]{1,0:T(8,128)(2,1)}, u32[]{:S(2)}, u32[]{:S(2)}) %collective-permute-start.2) | collective-permute-done | bytes 1835040 | tf_op jit(solution)/shard_map/ppermute | solution.py:253
  58.0 3.7 pad_maximum_fusion.3.tok_ref
  61.7 210.1 %expert_forward.1 = f32[2,448,2048]{2,1,0:T(8,128)} custom-call(s32[2,32]{1,0:T(2,128)} %slice_reduce_fusion.cnt_ref, s32[2,32,2048]{2,1,0:T(8,128)} %get-tuple-element.48.pos_ref, f32[2,32,2048]{2,1,0:T(8,128)} %get-tuple-element.49.gmat_ref, bf16[2,448,2048]{2,1,0:T(8,128)(2,1)} %pad_maximum_fusion.3.tok_ref, bf16[2,32,320,448]{3,2,1,0:T(8,128)(2,1)} %bitcast.285, ...), custom_call_target="tpu_custom_call" | custom-call | flops 74222403584 | bytes 27525120 | tf_op jit(solution)/shard_map/expert_forward/pallas_call | solution.py:116
  271.8 4.3 slice_bitcast_fusion
  276.1 12.2 collective-permute-start.3
  288.3 19.5 fusion.11
  307.8 13.1 fusion.49
  320.9 8.4 fusion.53
  333.8 4.4 pad_maximum_fusion.5.gy_ref
  338.2 28.6 %collective-permute-done.3 = f32[448,2048]{1,0:T(8,128)} collective-permute-done((f32[448,2048]{1,0:T(8,128)}, f32[448,2048]{1,0:T(8,128)}, u32[]{:S(2)}, u32[]{:S(2)}) %collective-permute-start.3) | collective-permute-done | bytes 3670048 | tf_op jit(solution)/shard_map/ppermute | solution.py:253
  366.8 4.6 fusion.33
  372.7 10.2 fusion.47
  385.5 30.3 %fusion.9 = (bf16[2560,2048]{0,1:T(8,128)(2,1)}, bf16[2560,2048]{0,1:T(8,128)(2,1)}, f32[2048,2560]{1,0:T(8,128)}) fusion(f32[2560,2048]{0,1:T(8,128)} %fusion.49, f32[2048,2560]{1,0:T(8,128)} %fusion.47, bf16[448,2048]{1,0:T(8,128)(2,1)S(1)} %fusion.38, bf16[2,448,2560]{2,1,0:T(8,128)(2,1)S(1)} %bitcast.296), kind=kOutput, calls=%fused_computation.16 | convolution fusion | flops 4765777920 | bytes 88014848 | tf_op jit(solution)/shard_map/dot_general | solution.py:17
  415.7 10.2 collective-permute-done.4
  428.1 366.7 %expert_backward.2 = (f32[448,2048]{1,0:T(8,128)}, bf16[448,2048]{1,0:T(8,128)(2,1)}, bf16[32,3360,128]{2,1,0:T(8,128)(2,1)}) custom-call(s32[2,32]{1,0:T(2,128)} %slice_reduce_fusion.1.cnt_ref, s32[2,32,2048]{2,1,0:T(8,128)} %get-tuple-element.45.pos_ref, f32[2,32,2048]{2,1,0:T(8,128)} %get-tuple-element.46.gmat_ref, ...), custom_call_target="tpu_custom_call" | custom-call | flops 132472897536 | bytes 55050240 | tf_op jit(solution)/shard_map/expert_backward/pallas_call | solution.py:196
  797.1 8.7 fusion.45
  805.8 7.8 fusion.41
  813.6 22.4 %collective-permute-done.6 = bf16[448,2048]{1,0:T(8,128)(2,1)S(1)} collective-permute-done((bf16[448,2048]{1,0:T(8,128)(2,1)}, bf16[448,2048]{1,0:T(8,128)(2,1)S(1)}, u32[]{:S(2)}, u32[]{:S(2)}) %collective-permute-start.6) | collective-permute-done | bytes 1835040 | tf_op jit(solution)/shard_map/ppermute | solution.py:253
  836.0 3.3 fusion.37
  843.1 13.3 constant_dynamic-slice_fusion.1
  857.4 25.9 %collective-permute-done.7 = bf16[448,2048]{1,0:T(8,128)(2,1)} collective-permute-done((bf16[448,2048]{1,0:T(8,128)(2,1)S(1)}, bf16[448,2048]{1,0:T(8,128)(2,1)}, u32[]{:S(2)}, u32[]{:S(2)}) %collective-permute-start.7) | collective-permute-done | bytes 1835040 | tf_op jit(solution)/shard_map/ppermute | solution.py:253
  883.3 3.7 pad_maximum_fusion.6.gy_ref
  887.0 358.0 %expert_backward.3 = (f32[448,2048]{1,0:T(8,128)}, bf16[448,2048]{1,0:T(8,128)(2,1)}, bf16[32,3360,128]{2,1,0:T(8,128)(2,1)}) custom-call(s32[2,32]{1,0:T(2,128)} %slice_reduce_fusion.cnt_ref, s32[2,32,2048]{2,1,0:T(8,128)} %get-tuple-element.48.pos_ref, f32[2,32,2048]{2,1,0:T(8,128)} %get-tuple-element.49.gmat_ref, ...), custom_call_target="tpu_custom_call" | custom-call | flops 132472897536 | bytes 55050240 | tf_op jit(solution)/shard_map/expert_backward/pallas_call | solution.py:196
  1245.0 13.4 constant_dynamic-slice_fusion.3
  1258.4 26.5 %collective-permute-start.9 = (bf16[16,3360,128]{2,1,0:T(8,128)(2,1)}, bf16[16,3360,128]{2,1,0:T(8,128)(2,1)}, u32[]{:S(2)}, u32[]{:S(2)}) collective-permute-start(bf16[16,3360,128]{2,1,0:T(8,128)(2,1)} %constant_dynamic-slice_fusion.3), channel_id=1, source_target_pairs={{0,1},{1,0},{2,3},{3,2},{4,5},{5,4},{6,7},{7,6}} | collective-permute-start | bytes 41287688 | tf_op jit(solution)/shard_map/ppermute | solution.py:253
  1284.9 10.6 fusion.23
  1295.5 6.2 fusion.25
  1301.7 18.4 fusion.27
  1320.0 11.1 add_convert_fusion
  1331.2 3.5 constant_dynamic-slice_fusion
  1334.7 3.5 copy-done
  1338.2 11.1 add_convert_fusion.1
  1349.3 3.6 constant_dynamic-slice_fusion.2
  1352.9 3.6 copy-done.1
  1358.6 26.3 %fusion.1 = (bf16[2560,2048]{0,1:T(8,128)(2,1)S(1)}, bf16[2560,2048]{0,1:T(8,128)(2,1)}) fusion(f32[2048,2560]{1,0:T(8,128)} %get-tuple-element.115, f32[2048,2560]{1,0:T(8,128)} %fusion.61, bf16[448,2048]{1,0:T(8,128)(2,1)} %copy-done.4, bf16[2,2560,448]{1,2,0:T(8,128)(2,1)} %param.21), kind=kOutput, calls=%fused_computation.5 | convolution fusion | flops 4765777920 | bytes 67043328 | tf_op jit(solution)/shard_map/dot_general | solution.py:17
  1384.9 14.0 fusion.26
  1398.8 6.1 fusion.22
  1405.0 84.2 %collective-permute-done.15 = bf16[8,3360,128]{2,1,0:T(8,128)(2,1)} collective-permute-done((bf16[8,3360,128]{2,1,0:T(8,128)(2,1)}, bf16[8,3360,128]{2,1,0:T(8,128)(2,1)}, u32[]{:S(2)}, u32[]{:S(2)}) %collective-permute-start.15) | collective-permute-done | bytes 6881312 | tf_op jit(solution)/shard_map/ppermute | solution.py:253
  1489.2 9.5 add_convert_fusion.2.pack_ref
  1498.7 138.0 %collective-permute-done.10 = bf16[8,3360,128]{2,1,0:T(8,128)(2,1)} collective-permute-done((bf16[8,3360,128]{2,1,0:T(8,128)(2,1)}, bf16[8,3360,128]{2,1,0:T(8,128)(2,1)}, u32[]{:S(2)}, u32[]{:S(2)}) %collective-permute-start.10) | collective-permute-done | bytes 6881312 | tf_op jit(solution)/shard_map/ppermute | solution.py:253
  1636.7 9.6 add_convert_fusion.3.pack_ref
  1646.2 10.4 fusion.24
  1656.7 8.5 fusion.55
  1667.2 7.8 fusion.59
  1675.0 30.8 %collective-permute-done.8 = bf16[448,2048]{1,0:T(8,128)(2,1)S(1)} collective-permute-done((bf16[448,2048]{1,0:T(8,128)(2,1)S(1)}, bf16[448,2048]{1,0:T(8,128)(2,1)S(1)}, u32[]{:S(2)}, u32[]{:S(2)}) %collective-permute-start.8) | collective-permute-done | bytes 1835040 | tf_op jit(solution)/shard_map/ppermute | solution.py:253
  1707.5 3.4 fusion.74
  1711.0 134.6 %collective-permute-done.16.pack_ref = bf16[8,3360,128]{2,1,0:T(8,128)(2,1)} collective-permute-done((bf16[8,3360,128]{2,1,0:T(8,128)(2,1)}, bf16[8,3360,128]{2,1,0:T(8,128)(2,1)}, u32[]{:S(2)}, u32[]{:S(2)}) %collective-permute-start.16) | collective-permute-done | bytes 6881312 | tf_op jit(solution)/shard_map/ppermute | solution.py:253
  1846.1 241.9 %collective-permute-done.11.pack_ref = bf16[8,3360,128]{2,1,0:T(8,128)(2,1)} collective-permute-done((bf16[8,3360,128]{2,1,0:T(8,128)(2,1)}, bf16[8,3360,128]{2,1,0:T(8,128)(2,1)}, u32[]{:S(2)}, u32[]{:S(2)}) %collective-permute-start.11) | collective-permute-done | bytes 6881312 | tf_op jit(solution)/shard_map/ppermute | solution.py:253
  2093.0 4.6 pad_maximum_fusion.2
  2099.0 4.0 pad_maximum_fusion
  2103.0 7.4 broadcast_5_refs_0__refs_1__refs_2_.2.refs_0_
  2110.4 7.4 broadcast_5_refs_0__refs_1__refs_2_.2.clone.refs_1_
  2117.7 7.4 broadcast_5_refs_0__refs_1__refs_2_.2.clone.1.refs_2_
  2125.1 8.5 unpack.8
  2133.5 8.5 unpack.9
  2142.0 8.5 unpack.10
  2150.5 8.5 unpack.11
  2158.9 8.5 unpack.12
  2167.4 8.5 unpack.13
  2175.9 8.5 unpack.14
  2184.3 8.5 unpack.15
  (122 shorter events, 39.1 us)
Async XLA Ops:
  7.2 2083.2 %all-reduce.3.cloned.1.call-start = ((), (), s32[]{:S(2)}) async-start(), calls=%async_computation | async-start | bytes 29360128 | tf_op jit(solution)/shard_map/psum | solution.py:331
  8.2 20.2 collective-permute-start
  11.6 5.6 slice-start.2
  11.6 5.6 slice-start.3
  11.6 16.1 collective-permute-start.1
  15.1 351.6 %copy-start.2 = (bf16[448,2048]{1,0:T(8,128)(2,1)}, bf16[448,2048]{1,0:T(8,128)(2,1)S(1)}, u32[]{:S(2)}) copy-start(bf16[448,2048]{1,0:T(8,128)(2,1)S(1)} %fusion.39) | copy-start | bytes 5505028
  15.1 42.9 %collective-permute-start.2 = (bf16[448,2048]{1,0:T(8,128)(2,1)S(1)}, bf16[448,2048]{1,0:T(8,128)(2,1)}, u32[]{:S(2)}, u32[]{:S(2)}) collective-permute-start(bf16[448,2048]{1,0:T(8,128)(2,1)S(1)} %fusion.39), channel_id=1, source_target_pairs={{0,4},{4,0},{1,5},{5,1},{2,6},{6,2},{3,7},{7,3}} | collective-permute-start | bytes 5505032 | tf_op jit(solution)/shard_map/ppermute | solution.py:253
  17.0 10.7 copy-start.21
  17.0 316.8 %collective-permute-start.5 = (bf16[448,2048]{1,0:T(8,128)(2,1)}, bf16[448,2048]{1,0:T(8,128)(2,1)}, u32[]{:S(2)}, u32[]{:S(2)}) collective-permute-start(bf16[448,2048]{1,0:T(8,128)(2,1)} %bitcast), channel_id=1, source_target_pairs={{0,4},{4,0},{1,5},{5,1},{2,6},{6,2},{3,7},{7,3}} | collective-permute-start | bytes 5505032 | tf_op jit(solution)/shard_map/ppermute | solution.py:253
  276.1 90.6 %collective-permute-start.3 = (f32[448,2048]{1,0:T(8,128)}, f32[448,2048]{1,0:T(8,128)}, u32[]{:S(2)}, u32[]{:S(2)}) collective-permute-start(f32[448,2048]{1,0:T(8,128)} %slice_bitcast_fusion), channel_id=1, source_target_pairs={{0,4},{4,0},{1,5},{5,1},{2,6},{6,2},{3,7},{7,3}} | collective-permute-start | bytes 11010056 | tf_op jit(solution)/shard_map/ppermute | solution.py:253
  307.8 13.1 copy-start.27
  332.2 34.6 %copy-start.7 = (f32[2048,448]{0,1:T(8,128)S(1)}, f32[2048,448]{0,1:T(8,128)}, u32[]{:S(2)}) copy-start(f32[2048,448]{0,1:T(8,128)} %fusion.53) | copy-start | bytes 11010052
  333.8 38.9 %slice-start = ((s8[4587520]{0:T(1024)(128)(4,1)}), s8[4194304]{0:T(1024)(128)(4,1)S(1)}, s32[]{:S(2)}) async-start(s8[4587520]{0:T(1024)(128)(4,1)} %bitcast.291), calls=%async_computation.1 | async-start | bytes 8388608
  338.2 33.2 %copy-start.24 = (bf16[2,448,448]{2,1,0:T(8,128)(2,1)S(1)}, bf16[2,448,448]{2,1,0:T(8,128)(2,1)}, u32[]{:S(2)}) copy-start(bf16[2,448,448]{2,1,0:T(8,128)(2,1)} %param.15) | copy-start | bytes 2408452
  338.2 34.5 %slice-start.1 = ((s8[4587520]{0:T(1024)(128)(4,1)}), s8[393216]{0:T(1024)(128)(4,1)S(1)}, s32[]{:S(2)}) async-start(s8[4587520]{0:T(1024)(128)(4,1)} %bitcast.291), calls=%async_computation.2 | async-start | bytes 786432
  371.4 1.2 copy-start.15
  371.4 14.0 slice-start.4
  372.7 53.3 %copy-start.17 = (bf16[448,2048]{1,0:T(8,128)(2,1)}, bf16[448,2048]{1,0:T(8,128)(2,1)S(1)}, u32[]{:S(2)}) copy-start(bf16[448,2048]{1,0:T(8,128)(2,1)S(1)} %fusion.38) | copy-start | bytes 5505028
  372.7 12.7 slice-start.5
  382.9 43.0 %collective-permute-start.4 = (bf16[448,2048]{1,0:T(8,128)(2,1)S(1)}, bf16[448,2048]{1,0:T(8,128)(2,1)S(1)}, u32[]{:S(2)}, u32[]{:S(2)}) collective-permute-start(bf16[448,2048]{1,0:T(8,128)(2,1)S(1)} %fusion.38), channel_id=1, source_target_pairs={{0,4},{4,0},{1,5},{5,1},{2,6},{6,2},{3,7},{7,3}} | collective-permute-start | bytes 5505032 | tf_op jit(solution)/shard_map/ppermute | solution.py:253
  794.8 41.2 %collective-permute-start.6 = (bf16[448,2048]{1,0:T(8,128)(2,1)}, bf16[448,2048]{1,0:T(8,128)(2,1)S(1)}, u32[]{:S(2)}, u32[]{:S(2)}) collective-permute-start(bf16[448,2048]{1,0:T(8,128)(2,1)} %get-tuple-element.51), channel_id=1, source_target_pairs={{0,4},{4,0},{1,5},{5,1},{2,6},{6,2},{3,7},{7,3}} | collective-permute-start | bytes 5505032 | tf_op jit(solution)/shard_map/ppermute | solution.py:253
  797.1 8.7 copy-start.22
  805.8 30.2 %copy-start.9 = (f32[448,2048]{1,0:T(8,128)S(1)}, f32[448,2048]{1,0:T(8,128)}, u32[]{:S(2)}) copy-start(f32[448,2048]{1,0:T(8,128)} %get-tuple-element.50) | copy-start | bytes 11010052
  836.0 3.3 copy-start.25
  839.3 1.2 copy-start.19
  840.6 42.7 %copy-start.4 = (bf16[448,2048]{1,0:T(8,128)(2,1)}, bf16[448,2048]{1,0:T(8,128)(2,1)S(1)}, u32[]{:S(2)}) copy-start(bf16[448,2048]{1,0:T(8,128)(2,1)S(1)} %fusion.36) | copy-start | bytes 5505028
  840.6 42.7 %collective-permute-start.7 = (bf16[448,2048]{1,0:T(8,128)(2,1)S(1)}, bf16[448,2048]{1,0:T(8,128)(2,1)}, u32[]{:S(2)}, u32[]{:S(2)}) collective-permute-start(bf16[448,2048]{1,0:T(8,128)(2,1)S(1)} %fusion.36), channel_id=1, source_target_pairs={{0,4},{4,0},{1,5},{5,1},{2,6},{6,2},{3,7},{7,3}} | collective-permute-start | bytes 5505032 | tf_op jit(solution)/shard_map/ppermute | solution.py:253
  856.3 463.7 %collective-permute-start.14 = (bf16[16,3360,128]{2,1,0:T(8,128)(2,1)}, bf16[16,3360,128]{2,1,0:T(8,128)(2,1)}, u32[]{:S(2)}, u32[]{:S(2)}) collective-permute-start(bf16[16,3360,128]{2,1,0:T(8,128)(2,1)} %constant_dynamic-slice_fusion.1), channel_id=1, source_target_pairs={{0,1},{1,0},{2,3},{3,2},{4,5},{5,4},{6,7},{7,6}} | collective-permute-start | bytes 41287688 | tf_op jit(solution)/shard_map/ppermute | solution.py:253
  1245.0 39.9 %copy-start.18 = (bf16[448,2048]{1,0:T(8,128)(2,1)S(1)}, bf16[448,2048]{1,0:T(8,128)(2,1)}, u32[]{:S(2)}) copy-start(bf16[448,2048]{1,0:T(8,128)(2,1)} %copy-done.17) | copy-start | bytes 5505028
  1258.4 79.7 %collective-permute-start.9 = (bf16[16,3360,128]{2,1,0:T(8,128)(2,1)}, bf16[16,3360,128]{2,1,0:T(8,128)(2,1)}, u32[]{:S(2)}, u32[]{:S(2)}) collective-permute-start(bf16[16,3360,128]{2,1,0:T(8,128)(2,1)} %constant_dynamic-slice_fusion.3), channel_id=1, source_target_pairs={{0,1},{1,0},{2,3},{3,2},{4,5},{5,4},{6,7},{7,6}} | collective-permute-start | bytes 41287688 | tf_op jit(solution)/shard_map/ppermute | solution.py:253
  1284.9 10.6 copy-start.28
  1331.2 7.0 copy-start
  1338.2 151.0 %collective-permute-start.15 = (bf16[8,3360,128]{2,1,0:T(8,128)(2,1)}, bf16[8,3360,128]{2,1,0:T(8,128)(2,1)}, u32[]{:S(2)}, u32[]{:S(2)}) collective-permute-start(bf16[8,3360,128]{2,1,0:T(8,128)(2,1)} %constant_dynamic-slice_fusion), channel_id=1, source_target_pairs={{0,2},{1,3},{2,0},{3,1},{4,6},{5,7},{6,4},{7,5}} | collective-permute-start | bytes 20643848 | tf_op jit(solution)/shard_map/ppermute | solution.py:253
  1349.3 7.2 copy-start.1
  1356.5 280.1 %collective-permute-start.10 = (bf16[8,3360,128]{2,1,0:T(8,128)(2,1)}, bf16[8,3360,128]{2,1,0:T(8,128)(2,1)}, u32[]{:S(2)}, u32[]{:S(2)}) collective-permute-start(bf16[8,3360,128]{2,1,0:T(8,128)(2,1)} %constant_dynamic-slice_fusion.2), channel_id=1, source_target_pairs={{0,2},{1,3},{2,0},{3,1},{4,6},{5,7},{6,4},{7,5}} | collective-permute-start | bytes 20643848 | tf_op jit(solution)/shard_map/ppermute | solution.py:253
  1358.6 26.3 %copy-start.5 = (bf16[448,2048]{1,0:T(8,128)(2,1)S(1)}, bf16[448,2048]{1,0:T(8,128)(2,1)}, u32[]{:S(2)}) copy-start(bf16[448,2048]{1,0:T(8,128)(2,1)} %copy-done.4) | copy-start | bytes 5505028
  1384.9 14.0 copy-start.29
  1384.9 14.0 copy-start.3
  1498.7 346.9 %collective-permute-start.16 = (bf16[8,3360,128]{2,1,0:T(8,128)(2,1)}, bf16[8,3360,128]{2,1,0:T(8,128)(2,1)}, u32[]{:S(2)}, u32[]{:S(2)}) collective-permute-start(bf16[8,3360,128]{2,1,0:T(8,128)(2,1)} %add_convert_fusion.2.pack_ref), channel_id=1, source_target_pairs={{0,2},{1,3},{2,0},{3,1},{4,6},{5,7},{6,4},{7,5}} | collective-permute-start | bytes 20643848 | tf_op jit(solution)/shard_map/ppermute | solution.py:253
  1646.2 441.7 %collective-permute-start.11 = (bf16[8,3360,128]{2,1,0:T(8,128)(2,1)}, bf16[8,3360,128]{2,1,0:T(8,128)(2,1)}, u32[]{:S(2)}, u32[]{:S(2)}) collective-permute-start(bf16[8,3360,128]{2,1,0:T(8,128)(2,1)} %add_convert_fusion.3.pack_ref), channel_id=1, source_target_pairs={{0,2},{1,3},{2,0},{3,1},{4,6},{5,7},{6,4},{7,5}} | collective-permute-start | bytes 20643848 | tf_op jit(solution)/shard_map/ppermute | solution.py:253
  1646.2 20.9 slice-start.6
  1656.7 8.5 copy-start.23
  1656.7 8.6 copy-start.16
  1656.7 8.6 copy-start.20
  1656.7 10.5 slice-start.7
  1665.2 40.6 %collective-permute-start.8 = (bf16[448,2048]{1,0:T(8,128)(2,1)S(1)}, bf16[448,2048]{1,0:T(8,128)(2,1)S(1)}, u32[]{:S(2)}, u32[]{:S(2)}) collective-permute-start(bf16[448,2048]{1,0:T(8,128)(2,1)S(1)} %copy-done.23), channel_id=1, source_target_pairs={{0,4},{4,0},{1,5},{5,1},{2,6},{6,2},{3,7},{7,3}} | collective-permute-start | bytes 5505032 | tf_op jit(solution)/shard_map/ppermute | solution.py:253
  1667.2 38.6 %copy-start.6 = (bf16[448,2048]{1,0:T(8,128)(2,1)S(1)}, bf16[448,2048]{1,0:T(8,128)(2,1)}, u32[]{:S(2)}) copy-start(bf16[448,2048]{1,0:T(8,128)(2,1)} %copy-done.4) | copy-start | bytes 5505028
  1667.2 38.6 %copy-start.8 = (f32[448,2048]{1,0:T(8,128)S(1)}, f32[448,2048]{1,0:T(8,128)}, u32[]{:S(2)}) copy-start(f32[448,2048]{1,0:T(8,128)} %get-tuple-element.52) | copy-start | bytes 11010052
  1710.9 377.1 %copy-start.26 = (bf16[2,448,448]{2,1,0:T(8,128)(2,1)S(1)}, bf16[2,448,448]{2,1,0:T(8,128)(2,1)}, u32[]{:S(2)}) copy-start(bf16[2,448,448]{2,1,0:T(8,128)(2,1)} %param.15) | copy-start | bytes 2408452
  1710.9 431.1 %collective-permute-start.18 = (bf16[8,3360,128]{2,1,0:T(8,128)(2,1)}, bf16[8,3360,128]{2,1,0:T(8,128)(2,1)}, u32[]{:S(2)}, u32[]{:S(2)}) collective-permute-start(bf16[8,3360,128]{2,1,0:T(8,128)(2,1)} %add_convert_fusion.2.pack_ref), channel_id=1, source_target_pairs={{0,1},{1,0},{2,3},{3,2},{4,5},{5,4},{6,7},{7,6}} | collective-permute-start | bytes 20643848 | tf_op jit(solution)/shard_map/ppermute | solution.py:253
  1845.6 304.9 %collective-permute-start.17 = (bf16[8,3360,128]{2,1,0:T(8,128)(2,1)}, bf16[8,3360,128]{2,1,0:T(8,128)(2,1)}, u32[]{:S(2)}, u32[]{:S(2)}) collective-permute-start(bf16[8,3360,128]{2,1,0:T(8,128)(2,1)} %collective-permute-done.16.pack_ref), channel_id=1, source_target_pairs={{0,1},{1,0},{2,3},{3,2},{4,5},{5,4},{6,7},{7,6}} | collective-permute-start | bytes 20643848 | tf_op jit(solution)/shard_map/ppermute | solution.py:253
  1845.6 330.3 %collective-permute-start.13 = (bf16[8,3360,128]{2,1,0:T(8,128)(2,1)}, bf16[8,3360,128]{2,1,0:T(8,128)(2,1)}, u32[]{:S(2)}, u32[]{:S(2)}) collective-permute-start(bf16[8,3360,128]{2,1,0:T(8,128)(2,1)} %add_convert_fusion.3.pack_ref), channel_id=1, source_target_pairs={{0,1},{1,0},{2,3},{3,2},{4,5},{5,4},{6,7},{7,6}} | collective-permute-start | bytes 20643848 | tf_op jit(solution)/shard_map/ppermute | solution.py:253
  2088.0 96.4 %collective-permute-start.12 = (bf16[8,3360,128]{2,1,0:T(8,128)(2,1)}, bf16[8,3360,128]{2,1,0:T(8,128)(2,1)}, u32[]{:S(2)}, u32[]{:S(2)}) collective-permute-start(bf16[8,3360,128]{2,1,0:T(8,128)(2,1)} %collective-permute-done.11.pack_ref), channel_id=1, source_target_pairs={{0,1},{1,0},{2,3},{3,2},{4,5},{5,4},{6,7},{7,6}} | collective-permute-start | bytes 20643848 | tf_op jit(solution)/shard_map/ppermute | solution.py:253
  2090.3 2.7 copy-start.14
  2093.0 4.6 copy-start.10
  2093.0 4.6 copy-start.11
  2093.0 4.9 copy-start.12
  2093.0 6.0 copy-start.13
Sparse Core Ops, SparseCore 0:
  1711.0 341.9 all-reduce.2
